TPU v7x, 32 devices: a whole 2x2x4 slice. The times are simulated.
32 devices in a mesh: scen: 8 (over z, x), rootr: 2 (over core), rootc: 2 (over y).
Axes of the slice: x: 2, y: 2, z: 4, core: 2. Of those that a mesh axis runs over, the one named last changes fastest.
Arguments:
- start_guess: float32 [8192, 256], P(('scen', 'rootr'), 'rootc'), may hold values from -6 to 6
- right_side: float32 [8192, 256], P(('scen', 'rootr'), 'rootc'), may hold values from -6 to 6
- root_diagonal: float32 [8192], P(('scen', 'rootr')), may hold values from 1 to 4
- preconditioner: bfloat16 [8192, 8192], P(('scen', 'rootr')), may hold values from -0.015625 to 0.015625
- border_block: bfloat16 [16, 512, 768], P(('scen', 'rootr'), 'rootc'), may hold values from -0.21875 to 0.21875
- coupling_inverse: bfloat16 [16, 512, 512], P(('scen', 'rootr'), 'rootc'), may hold values from -0.25 to 0.25
- border_count: int32 [16], P(('scen', 'rootr')), may hold values from 64 to 512, as said below
- column_tiles: int32 [16, 6], P(('scen', 'rootr')), may hold values from 0 to 63, as said below
Outputs:
- final_iterate: float32 [8192, 256], P(('scen', 'rootr'), 'rootc')
Inputs may be any that keep to these rules, and one draw needn't show every extreme that they name: A scenario's live border rows are its first border_count rows; some scenario has exactly 512. `column_tiles`: each row names 6 different tiles in rising order.
All inputs are finite; a program needn't handle non-finite values.
Results may differ from a plain program's by a relative error of at most 0.0022.
Values may be sent and summed in bfloat16 or wider, within the bound.
A program may use at most 64 MiB of HBM per device.

v0:
```python
import jax
import jax.numpy as jnp
from jax import lax
from jax.sharding import PartitionSpec as P

TILE = 128


def border_product(matrix, operand, live_here):
    half_rows = matrix.shape[0]
    live_mask = (jnp.arange(half_rows) < live_here)[:, None]
    product = jnp.dot(matrix, operand, preferred_element_type=jnp.float32)
    return jnp.where(live_mask, product, 0.0).astype(jnp.bfloat16)


def border_transpose(border, solved):
    numbers = (((0,), (0,)), ((), ()))
    return lax.dot_general(border, solved, numbers, preferred_element_type=jnp.float32)


def local(
    start_guess,
    right_side,
    root_diagonal,
    preconditioner,
    border_block,
    coupling_inverse,
    border_count,
    column_tiles,
):
    own_rows = start_guess.shape[0]
    half_rhs = start_guess.shape[1]
    half_rows = border_block.shape[1]
    coupled_cols = border_block.shape[2]
    order_rows = preconditioner.shape[1]
    border = border_block[0]
    inverse_rows = coupling_inverse[0]
    tile_ids = column_tiles[0]
    offset = lax.axis_index("rootc") * half_rows
    live_here = jnp.clip(border_count[0] - offset, 0, half_rows)
    iterate = start_guess
    own_low = iterate.astype(jnp.bfloat16)
    both_halves = lax.all_gather(own_low, "rootc", axis=1, tiled=True)
    gathered = lax.all_gather(both_halves, ("scen", "rootr"), axis=0, tiled=True)
    all_rhs = gathered.shape[1]
    picked = gathered.reshape(order_rows // TILE, TILE, all_rhs)[tile_ids].reshape(
        coupled_cols, all_rhs
    )
    values_local = border_product(border, picked, live_here)
    values_whole = lax.all_gather(values_local, "rootc", axis=0, tiled=True)
    solved = border_product(inverse_rows, values_whole, live_here)
    term_part = border_transpose(border, solved)
    term_half = lax.psum_scatter(term_part, "rootc", scatter_dimension=1, tiled=True)
    spread_terms = jnp.zeros((order_rows // TILE, TILE, half_rhs), jnp.float32)
    spread_terms = (
        spread_terms.at[tile_ids]
        .add(term_half.reshape(-1, TILE, half_rhs))
        .reshape(order_rows, half_rhs)
    )
    own_terms = right_side - root_diagonal[:, None] * iterate
    first_row = lax.axis_index(("scen", "rootr")) * own_rows
    current = lax.dynamic_slice_in_dim(spread_terms, first_row, own_rows, 0)
    spread_terms = lax.dynamic_update_slice_in_dim(spread_terms, current + own_terms, first_row, 0)
    residual = lax.psum(spread_terms, ("scen", "rootr"))
    update = jnp.dot(
        preconditioner, residual.astype(jnp.bfloat16), preferred_element_type=jnp.float32
    )
    iterate = iterate + update
    return iterate


def solution(mesh):
    placed = (
        P(("scen", "rootr"), "rootc"),
        P(("scen", "rootr"), "rootc"),
        P(("scen", "rootr")),
        P(("scen", "rootr"), None),
        P(("scen", "rootr"), "rootc", None),
        P(("scen", "rootr"), "rootc", None),
        P(("scen", "rootr")),
        P(("scen", "rootr"), None),
    )
    return jax.shard_map(
        local, mesh=mesh, in_specs=placed, out_specs=P(("scen", "rootr"), "rootc"), check_vma=False
    )
```

profile of v0, /device:TPU:1, one launch (start us, length us, event | category | flops | bytes accessed | tf_op | source)
XLA Modules:
  0.0 212.2 jit_solution(9271630107999515381)
XLA Ops:
  6.5 0.0 copy-start
  6.5 0.0 copy-start.1
  6.5 0.0 all-gather.2.cloned.1.call-start
  6.5 1.0 convert_element_type.16
  7.6 6.1 %all_gather.9 = bf16[512,256]{1,0:T(8,128)(2,1)} all-gather(bf16[512,128]{1,0:T(8,128)(2,1)S(1)} %convert_element_type.16), channel_id=1, replica_groups=mesh['scen'=8,'rootr'=2,'rootc'=2] {'rootc'}, dimensions={1}, use_global_device_ids=true | all-gather | bytes 393216 | tf_op jit(solution)/shard_map/all_gather | solution.py:43
  13.6 0.0 all-gather.2.cloned.1.call-update
  13.7 0.0 reduce-scatter.2.cloned.1.call-start
  14.4 0.7 fusion.17
  15.0 51.6 %all-gather.2.cloned.1.call-done = bf16[8192,256]{1,0:T(8,128)(2,1)} async-done(((bf16[512,256]{1,0:T(8,128)(2,1)}), bf16[8192,256]{1,0:T(8,128)(2,1)}) %all-gather.2.cloned.1.call-update) | async-done | bytes 4194320 | tf_op jit(solution)/shard_map/all_gather | solution.py:44
  66.7 2.8 %gather_fusion = bf16[6,128,256]{2,1,0:T(8,128)(2,1)S(1)} fusion(bf16[64,128,256]{2,1,0:T(8,128)(2,1)} %bitcast.34, s32[1024]{0:T(1024)S(1)} %pad_clamp_fusion), kind=kCustom, calls=%fused_computation | custom fusion | bytes 786456 | tf_op jit(solution)/shard_map/gather | solution.py:46
  69.4 0.0 copy-done
  69.4 0.3 fusion.10
  69.8 5.4 %all_gather.11 = bf16[512,256]{0,1:T(8,128)(2,1)S(1)} all-gather(bf16[256,256]{0,1:T(8,128)(2,1)S(1)} %fusion.10), channel_id=1, replica_groups=mesh['scen'=8,'rootr'=2,'rootc'=2] {'rootc'}, dimensions={0}, use_global_device_ids=true | all-gather | bytes 393216 | tf_op jit(solution)/shard_map/all_gather | solution.py:50
  75.2 0.0 copy-start.2
  75.2 0.0 copy-start.3
  75.2 2.4 %convolution_bitcast_fusion = f32[768,256]{0,1:T(8,128)} fusion(bf16[512,256]{0,1:T(8,128)(2,1)S(1)} %all_gather.11, bf16[1,256,768]{2,1,0:T(8,128)(2,1)S(1)} %copy-done, bf16[1,256,512]{2,1,0:T(8,128)(2,1)} %param.13, pred[256]{0:T(512)(128)(4,1)S(1)} %iota_compare_fusion), kind=kOutput, calls=%fused_computation.4 | convolution fusion | flops 167903232 | bytes 1704192 | tf_op jit(solution)/shard_map/dot_general | solution.py:18
  77.7 0.0 reduce-scatter.2.cloned.1.call-update
  77.7 0.0 copy-done.1
  77.7 0.1 copy.12
  77.8 16.3 %reduce-scatter.2.cloned.1.call-done = f32[768,128]{0,1:T(8,128)} async-done(((f32[768,256]{0,1:T(8,128)}), f32[768,128]{0,1:T(8,128)}) %reduce-scatter.2.cloned.1.call-update) | async-done | bytes 393232 | tf_op jit(solution)/shard_map/reduce_scatter | solution.py:53
  94.2 1.1 copy.11
  95.3 2.5 %broadcast_in_dim.24 = f32[64,128,128]{2,1,0:T(8,128)} broadcast(f32[]{:T(128)} %constant.10.clone.1), dimensions={} | broadcast | bytes 4194308 | tf_op jit(solution)/shard_map/broadcast_in_dim | solution.py:54
  97.8 2.6 %scatter_fusion = f32[64,128,128]{2,1,0:T(8,128)} fusion(f32[64,128,128]{2,1,0:T(8,128)} %broadcast_in_dim.24, s32[6]{0:T(128)S(1)} %fusion.17, f32[6,128,128]{2,1,0:T(8,128)S(1)} %bitcast.32), kind=kCustom, calls=%fused_computation.1 | custom fusion | flops 98304 | bytes 1179672 | tf_op jit(solution)/shard_map/scatter-add | solution.py:57
  100.4 0.0 copy-done.2
  100.4 0.0 copy-done.3
  100.4 1.8 add_dynamic-update-slice_fusion
  102.1 96.1 %all-reduce.1 = bf16[8192,128]{1,0:T(8,128)(2,1)S(1)} all-reduce(f32[8192,128]{1,0:T(8,128)} %add_dynamic-update-slice_fusion), channel_id=1, replica_groups=mesh['scen'=8,'rootr'=2,'rootc'=2] {'scen','rootr'}, use_global_device_ids=true, to_apply=%region_2.3 | all-reduce | flops 1048576 | bytes 6291456 | tf_op jit(solution)/shard_map/psum | solution.py:64
  198.2 6.3 %fusion.5 = f32[512,128]{0,1:T(8,128)S(1)} fusion(f32[512,128]{0,1:T(8,128)S(1)} %copy.12, bf16[512,8192]{1,0:T(8,128)(2,1)} %param.11, bf16[8192,128]{1,0:T(8,128)(2,1)S(1)} %all-reduce.1), kind=kOutput, calls=%fused_computation.8 | convolution fusion | flops 1073807360 | bytes 11010048 | tf_op jit(solution)/shard_map/dot_general | solution.py:65
  204.5 0.8 copy.13
  (2 shorter events, 0.0 us)
Async XLA Ops:
  6.5 62.9 %copy-start = (bf16[1,256,768]{2,1,0:T(8,128)(2,1)S(1)}, bf16[1,256,768]{2,1,0:T(8,128)(2,1)}, u32[]{:S(2)}) copy-start(bf16[1,256,768]{2,1,0:T(8,128)(2,1)} %param.12) | copy-start | bytes 1179652
  6.5 71.1 %copy-start.1 = (f32[512,128]{1,0:T(8,128)S(1)}, f32[512,128]{1,0:T(8,128)}, u32[]{:S(2)}) copy-start(f32[512,128]{1,0:T(8,128)} %param.8) | copy-start | bytes 786436
  6.5 60.1 %all-gather.2.cloned.1.call-start = ((), (), s32[]{:S(2)}) async-start(), calls=%async_computation.1 | async-start | bytes 4456448 | tf_op jit(solution)/shard_map/all_gather | solution.py:44
  13.7 80.5 %reduce-scatter.2.cloned.1.call-start = ((), (), s32[]{:S(2)}) async-start(), calls=%async_computation.2 | async-start | bytes 1179648 | tf_op jit(solution)/shard_map/reduce_scatter | solution.py:53
  75.2 25.2 %copy-start.2 = (f32[512,128]{1,0:T(8,128)S(1)}, f32[512,128]{1,0:T(8,128)}, u32[]{:S(2)}) copy-start(f32[512,128]{1,0:T(8,128)} %param.9) | copy-start | bytes 786436
  75.2 25.2 %copy-start.3 = (f32[512]{0:T(512)S(1)}, f32[512]{0:T(512)}, u32[]{:S(2)}) copy-start(f32[512]{0:T(512)} %param.10) | copy-start | bytes 6148
Sparse Core Ops, SparseCore 0:
  13.8 52.8 all-gather.1
  77.8 16.3 reduce-scatter.1
where the time goes:
time: 213 us; the launch traced here: 212 us
  blocking collectives  108 us (51%)
  waiting for transfers between devices  68 us (32%)
  between operations  14.1 us (7%)
  matrix products  9.04 us (4%)
  local copies, waits for them, and re-layouts  7.34 us (3%)
  other arithmetic  6.06 us (3%)
    psum x1, blocking collectives, local(): residual = lax.psum(spread_terms, ('scen', 'rootr'))  96.1 us
    all_gather x1, waiting for transfers between devices, local(): lax.all_gather(both_halves, ('scen', 'rootr'), axis=0, tiled=True)  51.6 us
    reduce_scatter x1, waiting for transfers between devices, local(): lax.psum_scatter(term_part, 'rootc', scatter_dimension=1, tiled=True)  16.3 us
    dot_general x1, matrix products, local(): jnp.dot(preconditioner, residual.astype(jnp.bfloat16), preferred_element_...  6.28 us
    all_gather x1, blocking collectives, local(): both_halves = lax.all_gather(own_low, 'rootc', axis=1, tiled=True)  6.05 us
    all_gather x1, blocking collectives, local(): values_whole = lax.all_gather(values_local, 'rootc', axis=0, tiled=True)  5.45 us
  transfers between devices with their start and end apart: 2, of which 2 were waited for; matrix products, arithmetic and copies ran while one was open for 0% of the time, Pallas kernels for 0%

commit v1 on v0

--- a/solution.py
+++ b/solution.py
@@ -61,7 +61,7 @@
     first_row = lax.axis_index(("scen", "rootr")) * own_rows
     current = lax.dynamic_slice_in_dim(spread_terms, first_row, own_rows, 0)
     spread_terms = lax.dynamic_update_slice_in_dim(spread_terms, current + own_terms, first_row, 0)
-    residual = lax.psum(spread_terms, ("scen", "rootr"))
+    residual = lax.psum(lax.psum(spread_terms, "rootr"), "scen")
     update = jnp.dot(
         preconditioner, residual.astype(jnp.bfloat16), preferred_element_type=jnp.float32
     )

time: 213 us -> 313 us (1.47)
  blocking collectives: 108 us -> 179 us
  waiting for transfers between devices: 68 us -> 96.8 us
    psum x1, blocking collectives: 96.1 us -> 167 us  [local(): residual = lax.psum(lax.psum(spread_terms, 'rootr'), 'scen')]
    psum x0 -> x1, waiting for transfers between devices: none -> 28.7 us  [local(): residual = lax.psum(lax.psum(spread_terms, 'rootr'), 'scen')]
  transfers between devices with their start and end apart: 2 -> 3, of which waited for: 2 -> 3; matrix products, arithmetic and copies ran while one was open for 0% -> 0% of each run, Pallas kernels for 0% -> 0%
where the time goes in v1:
time: 313 us; the launch traced here: 312 us
  blocking collectives  179 us (57%)
  waiting for transfers between devices  96.8 us (31%)
  between operations  13.8 us (4%)
  matrix products  9.05 us (3%)
  local copies, waits for them, and re-layouts  7.37 us (2%)
  other arithmetic  6.06 us (2%)
    psum x1, blocking collectives, local(): residual = lax.psum(lax.psum(spread_terms, 'rootr'), 'scen')  167 us
    all_gather x1, waiting for transfers between devices, local(): lax.all_gather(both_halves, ('scen', 'rootr'), axis=0, tiled=True)  51.6 us
    psum x1, waiting for transfers between devices, local(): residual = lax.psum(lax.psum(spread_terms, 'rootr'), 'scen')  28.7 us
    reduce_scatter x1, waiting for transfers between devices, local(): lax.psum_scatter(term_part, 'rootc', scatter_dimension=1, tiled=True)  16.4 us
    dot_general x1, matrix products, local(): jnp.dot(preconditioner, residual.astype(jnp.bfloat16), preferred_element_...  6.28 us
  transfers between devices with their start and end apart: 3, of which 3 were waited for; matrix products, arithmetic and copies ran while one was open for 0% of the time, Pallas kernels for 0%

profile of v1, /device:TPU:1, one launch (start us, length us, event | category | flops | bytes accessed | tf_op | source)
XLA Modules:
  0.0 311.7 jit_solution(3829483338112859500)
XLA Ops:
  6.5 0.0 copy-start
  6.5 0.0 all-gather.2.cloned.1.call-start
  6.5 1.0 convert_element_type.16
  7.6 6.1 %all_gather.9 = bf16[512,256]{1,0:T(8,128)(2,1)} all-gather(bf16[512,128]{1,0:T(8,128)(2,1)S(1)} %convert_element_type.16), channel_id=1, replica_groups=mesh['scen'=8,'rootr'=2,'rootc'=2] {'rootc'}, dimensions={1}, use_global_device_ids=true | all-gather | bytes 393216 | tf_op jit(solution)/shard_map/all_gather | solution.py:43
  13.6 0.0 all-gather.2.cloned.1.call-update
  13.6 0.0 reduce-scatter.2.cloned.1.call-start
  14.4 0.7 fusion.17
  15.0 51.6 %all-gather.2.cloned.1.call-done = bf16[8192,256]{1,0:T(8,128)(2,1)} async-done(((bf16[512,256]{1,0:T(8,128)(2,1)}), bf16[8192,256]{1,0:T(8,128)(2,1)}) %all-gather.2.cloned.1.call-update) | async-done | bytes 4194320 | tf_op jit(solution)/shard_map/all_gather | solution.py:44
  66.6 2.8 gather_fusion
  69.4 0.0 copy-done
  69.4 0.3 fusion.10
  69.7 5.4 %all_gather.11 = bf16[512,256]{0,1:T(8,128)(2,1)S(1)} all-gather(bf16[256,256]{0,1:T(8,128)(2,1)S(1)} %fusion.10), channel_id=1, replica_groups=mesh['scen'=8,'rootr'=2,'rootc'=2] {'rootc'}, dimensions={0}, use_global_device_ids=true | all-gather | bytes 393216 | tf_op jit(solution)/shard_map/all_gather | solution.py:50
  75.2 0.0 copy-start.1
  75.2 0.0 copy-start.2
  75.2 0.0 copy-start.3
  75.2 2.5 convolution_bitcast_fusion
  77.7 0.0 reduce-scatter.2.cloned.1.call-update
  77.7 0.0 all-reduce.3.cloned.1.call-start
  77.7 16.4 %reduce-scatter.2.cloned.1.call-done = f32[768,128]{0,1:T(8,128)} async-done(((f32[768,256]{0,1:T(8,128)}), f32[768,128]{0,1:T(8,128)}) %reduce-scatter.2.cloned.1.call-update) | async-done | bytes 393232 | tf_op jit(solution)/shard_map/reduce_scatter | solution.py:53
  94.2 1.1 copy.11
  95.3 2.5 broadcast_in_dim.24
  97.8 2.6 scatter_fusion
  100.4 0.0 copy-done.1
  100.4 0.0 copy-done.2
  100.4 0.0 copy-done.3
  100.4 1.8 add_dynamic-update-slice_fusion
  102.2 0.0 all-reduce.3.cloned.1.call-update
  102.2 0.1 copy.12
  102.4 28.7 %all-reduce.3.cloned.1.call-done = f32[8192,128]{1,0:T(8,128)} async-done(((f32[8192,128]{1,0:T(8,128)}), f32[8192,128]{1,0:T(8,128)}) %all-reduce.3.cloned.1.call-update) | async-done | bytes 4194320 | tf_op jit(solution)/shard_map/psum | solution.py:64
  131.0 167.0 %all-reduce.4 = bf16[8192,128]{1,0:T(8,128)(2,1)S(1)} all-reduce(f32[8192,128]{1,0:T(8,128)} %all-reduce.3.cloned.1.call-done), channel_id=1, replica_groups=mesh['scen'=8,'rootr'=2,'rootc'=2] {'scen'}, use_global_device_ids=true, to_apply=%region_3.4 | all-reduce | flops 1048576 | bytes 6291456 | tf_op jit(solution)/shard_map/psum | solution.py:64
  298.1 6.3 %fusion.5 = f32[512,128]{0,1:T(8,128)S(1)} fusion(f32[512,128]{0,1:T(8,128)S(1)} %copy.12, bf16[512,8192]{1,0:T(8,128)(2,1)} %param.11, bf16[8192,128]{1,0:T(8,128)(2,1)S(1)} %all-reduce.4), kind=kOutput, calls=%fused_computation.8 | convolution fusion | flops 1073807360 | bytes 11010048 | tf_op jit(solution)/shard_map/dot_general | solution.py:65
  304.3 0.8 copy.13
  (2 shorter events, 0.0 us)
Async XLA Ops:
  6.5 62.9 %copy-start = (bf16[1,256,768]{2,1,0:T(8,128)(2,1)S(1)}, bf16[1,256,768]{2,1,0:T(8,128)(2,1)}, u32[]{:S(2)}) copy-start(bf16[1,256,768]{2,1,0:T(8,128)(2,1)} %param.12) | copy-start | bytes 1179652
  6.5 60.1 %all-gather.2.cloned.1.call-start = ((), (), s32[]{:S(2)}) async-start(), calls=%async_computation.1 | async-start | bytes 4456448 | tf_op jit(solution)/shard_map/all_gather | solution.py:44
  13.6 80.5 %reduce-scatter.2.cloned.1.call-start = ((), (), s32[]{:S(2)}) async-start(), calls=%async_computation.2 | async-start | bytes 1179648 | tf_op jit(solution)/shard_map/reduce_scatter | solution.py:53
  75.2 25.2 %copy-start.1 = (f32[512,128]{1,0:T(8,128)S(1)}, f32[512,128]{1,0:T(8,128)}, u32[]{:S(2)}) copy-start(f32[512,128]{1,0:T(8,128)} %param.8) | copy-start | bytes 786436
  75.2 25.2 %copy-start.2 = (f32[512,128]{1,0:T(8,128)S(1)}, f32[512,128]{1,0:T(8,128)}, u32[]{:S(2)}) copy-start(f32[512,128]{1,0:T(8,128)} %param.9) | copy-start | bytes 786436
  75.2 25.2 %copy-start.3 = (f32[512]{0:T(512)S(1)}, f32[512]{0:T(512)}, u32[]{:S(2)}) copy-start(f32[512]{0:T(512)} %param.10) | copy-start | bytes 6148
  77.7 53.4 %all-reduce.3.cloned.1.call-start = ((), (), s32[]{:S(2)}) async-start(), calls=%async_computation.3 | async-start | bytes 8388608 | tf_op jit(solution)/shard_map/psum | solution.py:64
Sparse Core Ops, SparseCore 0:
  13.8 52.8 all-gather.1
  77.8 16.3 reduce-scatter.1
  102.3 28.6 all-reduce.2
